TPU v7x, 256 devices: a whole 4x4x8 slice. The times are simulated.
256 devices in a mesh: blk: 32 (over x, z), src: 2 (over y_lo), layer: 4 (over y_hi, core).
Axes of the slice: x: 4, y: 4 (y_hi: 2, y_lo: 2; y = y_hi * 2 + y_lo), z: 8, core: 2. Of those that a mesh axis runs over, the one named last changes fastest.
Arguments:
- resident_act: bfloat16 [4, 16384, 4096], P('layer', 'blk'), may hold values from -6 to 6
- resident_grad: bfloat16 [4, 16384, 4096], P('layer', 'blk'), may hold values from -6 to 6
- source_act: bfloat16 [4, 1024, 4096], P('layer', ('blk', 'src')), may hold values from -6 to 6
- source_grad: bfloat16 [4, 1024, 4096], P('layer', ('blk', 'src')), may hold values from -6 to 6
- probes: bfloat16 [1024, 256], P(('blk', 'src')), may hold values from -6 to 6
Outputs:
- kernel_product: float32 [16384, 256], P(('blk', 'layer'))
All inputs are finite; a program needn't handle non-finite values.
Results may differ from a plain program's by a relative error of at most 0.0029.
Values may be sent and summed in bfloat16 or wider, within the bound.
No kernel may reach another device: no remote copies, remote signals or barrier semaphores. Data moves between devices by JAX's collectives and lax.ppermute only.
A program may use at most 64 MiB of HBM per device.

v0:
```python
import jax
import jax.numpy as jnp
from jax import lax
from jax.sharding import PartitionSpec as P

LAYERS = 4


def contract_rows(left, right):
    return lax.dot_general(
        left, right, (((1,), (1,)), ((), ())), preferred_element_type=jnp.float32
    )


def on_device(resident_act, resident_grad, source_act, source_grad, probes):
    width = resident_act.shape[2]
    blocks = lax.axis_size("blk")
    source_total = source_act.shape[1] * blocks * lax.axis_size("src")
    inverse_width = jnp.float32(1.0 / width)
    probe_rows = lax.all_gather(probes, "blk", axis=0, tiled=True)
    acts = lax.all_gather(source_act[0], "blk", axis=0, tiled=True)
    grads = lax.all_gather(source_grad[0], "blk", axis=0, tiled=True)
    act_gram = contract_rows(acts, resident_act[0])
    grad_gram = contract_rows(grads, resident_grad[0])
    kernel = (act_gram * grad_gram * inverse_width).astype(jnp.bfloat16)
    total = lax.dot_general(
        kernel, probe_rows, (((0,), (0,)), ((), ())), preferred_element_type=jnp.float32
    )
    part = lax.psum_scatter(total, "layer", scatter_dimension=0, tiled=True)
    result = lax.psum(part, "src")
    return result * jnp.float32((LAYERS * source_total) ** (-0.5))


def solution(mesh):
    in_specs = (
        P("layer", "blk", None),
        P("layer", "blk", None),
        P("layer", ("blk", "src"), None),
        P("layer", ("blk", "src"), None),
        P(("blk", "src"), None),
    )
    out_specs = P(("blk", "layer"), None)
    return jax.shard_map(
        on_device, mesh=mesh, in_specs=in_specs, out_specs=out_specs, check_vma=False
    )
```

profile of v0, /device:TPU:1, one launch (start us, length us, event | category | flops | bytes accessed | tf_op | source)
XLA Modules:
  0.0 257.1 jit_solution(9820898550968278613)
XLA Ops:
  6.5 0.0 all-gather.7.cloned.1.call-start
  6.5 0.7 all-gather.7.cloned.1.call-update
  7.3 0.0 all-gather.5.cloned.1.call-start
  7.3 0.7 all-gather.5.cloned.1.call-update
  8.0 0.0 reduce-scatter.2.cloned.1.call-start
  8.1 42.0 %all_gather.11 = bf16[512,256]{1,0:T(8,128)(2,1)S(1)} all-gather(bf16[16,256]{1,0:T(8,128)(2,1)} %param.9), channel_id=1, replica_groups=mesh['blk'=32,'src'=2,'layer'=4] {'blk'}, dimensions={0}, use_global_device_ids=true | all-gather | bytes 270336 | tf_op jit(solution)/shard_map/all_gather | solution.py:20
  50.0 41.9 %all-gather.7.cloned.1.call-done = bf16[1,512,4096]{2,1,0:T(8,128)(2,1)} async-done(((bf16[1,16,4096]{2,1,0:T(8,128)(2,1)}), bf16[1,512,4096]{2,1,0:T(8,128)(2,1)}) %all-gather.7.cloned.1.call-update) | async-done | bytes 4194320 | tf_op jit(solution)/shard_map/all_gather | solution.py:22
  91.9 5.8 %fusion = f32[512,512]{1,0:T(8,128)S(1)} fusion(bf16[1,512,4096]{2,1,0:T(8,128)(2,1)} %param.6, bf16[1,512,4096]{2,1,0:T(8,128)(2,1)} %all-gather.7.cloned.1.call-done), kind=kOutput, calls=%fused_computation | convolution fusion | flops 2147483648 | bytes 9437184 | tf_op jit(solution)/shard_map/dot_general | solution.py:10
  97.8 75.3 %all-gather.5.cloned.1.call-done = bf16[1,512,4096]{2,1,0:T(8,128)(2,1)} async-done(((bf16[1,16,4096]{2,1,0:T(8,128)(2,1)}), bf16[1,512,4096]{2,1,0:T(8,128)(2,1)}) %all-gather.5.cloned.1.call-update) | async-done | bytes 4194320 | tf_op jit(solution)/shard_map/all_gather | solution.py:21
  173.0 7.1 %fusion.23 = f32[512,256]{1,0:T(8,128)} fusion(bf16[512,256]{1,0:T(8,128)(2,1)S(1)} %all_gather.11, f32[512,512]{1,0:T(8,128)S(1)} %fusion, bf16[1,512,4096]{2,1,0:T(8,128)(2,1)} %param.5, bf16[1,512,4096]{2,1,0:T(8,128)(2,1)} %all-gather.5.cloned.1.call-done), kind=kOutput, calls=%fused_computation.9 | convolution fusion | flops 2282487808 | bytes 10223616 | tf_op jit(solution)/shard_map/dot_general | solution.py:26
  180.1 0.0 reduce-scatter.2.cloned.1.call-update
  180.1 0.0 all-reduce.2.cloned.1.call-start
  180.2 34.0 %reduce-scatter.2.cloned.1.call-done = f32[128,256]{1,0:T(8,128)} async-done(((f32[512,256]{1,0:T(8,128)}), f32[128,256]{1,0:T(8,128)}) %reduce-scatter.2.cloned.1.call-update) | async-done | bytes 131088 | tf_op jit(solution)/shard_map/reduce_scatter | solution.py:29
  214.2 0.0 all-reduce.2.cloned.1.call-update
  214.2 34.8 %all-reduce.2.cloned.1.call-done = f32[128,256]{1,0:T(8,128)} async-done(((f32[128,256]{1,0:T(8,128)}), f32[128,256]{1,0:T(8,128)}) %all-reduce.2.cloned.1.call-update) | async-done | bytes 131088 | tf_op jit(solution)/shard_map/psum | solution.py:30
  249.0 1.6 broadcast_multiply_fusion
Async XLA Ops:
  6.5 85.4 %all-gather.7.cloned.1.call-start = ((), (), s32[]{:S(2)}) async-start(), calls=%async_computation.4 | async-start | bytes 4325376 | tf_op jit(solution)/shard_map/all_gather | solution.py:22
  7.3 165.8 %all-gather.5.cloned.1.call-start = ((), (), s32[]{:S(2)}) async-start(), calls=%async_computation.3 | async-start | bytes 4325376 | tf_op jit(solution)/shard_map/all_gather | solution.py:21
  8.0 206.1 %reduce-scatter.2.cloned.1.call-start = ((), (), s32[]{:S(2)}) async-start(), calls=%async_computation.1 | async-start | bytes 655360 | tf_op jit(solution)/shard_map/reduce_scatter | solution.py:29
  180.1 68.9 %all-reduce.2.cloned.1.call-start = ((), (), s32[]{:S(2)}) async-start(), calls=%async_computation.2 | async-start | bytes 262144 | tf_op jit(solution)/shard_map/psum | solution.py:30
Sparse Core Ops, SparseCore 0:
  9.9 81.9 all-gather.6
  94.5 78.4 all-gather.4
  180.3 33.8 reduce-scatter.1
  216.6 32.3 all-reduce.1
where the time goes:
time: 257 us
  waiting for transfers between devices  187 us (73%)
  blocking collectives  42 us (16%)
  between operations  13.1 us (5%)
  matrix products  12.9 us (5%)
    all_gather x1, waiting for transfers between devices, on_device(): acts = lax.all_gather(source_act[0], 'blk', axis=0, tiled=True)  75.3 us
    all_gather x1, blocking collectives, on_device(): probe_rows = lax.all_gather(probes, 'blk', axis=0, tiled=True)  42 us
    all_gather x1, waiting for transfers between devices, on_device(): grads = lax.all_gather(source_grad[0], 'blk', axis=0, tiled=True)  41.9 us
    psum x1, waiting for transfers between devices, on_device(): result = lax.psum(part, 'src')  34.8 us
    reduce_scatter x1, waiting for transfers between devices, on_device(): part = lax.psum_scatter(total, 'layer', scatter_dimension=0, tiled=True)  34 us
    dot_general x1, matrix products, on_device(): lax.dot_general(kernel, probe_rows, (((0,), (0,)), ((), ())), preferred_e...  7.07 us
    dot_general x1, matrix products, contract_rows(): lax.dot_general(left, right, (((1,), (1,)), ((), ())), preferred_element_...  5.82 us
  transfers between devices with their start and end apart: 4, of which 4 were waited for; matrix products, arithmetic and copies ran while one was open for 2% of the time, Pallas kernels for 0%

commit v1 on v0

--- a/solution.py
+++ b/solution.py
@@ -27,7 +27,7 @@
         kernel, probe_rows, (((0,), (0,)), ((), ())), preferred_element_type=jnp.float32
     )
     part = lax.psum_scatter(total, "layer", scatter_dimension=0, tiled=True)
-    result = lax.psum(part, "src")
+    result = jnp.sum(lax.all_gather(part, "src"), axis=0)
     return result * jnp.float32((LAYERS * source_total) ** (-0.5))
 
 

time: 257 us -> 227 us (0.88)
  waiting for transfers between devices: 187 us -> 153 us
  blocking collectives: 42 us -> 47.1 us
    psum x1 -> x0, waiting for transfers between devices: 34.8 us -> none  [on_device(): result = lax.psum(part, 'src')]
    all_gather x0 -> x1, blocking collectives: none -> 5.08 us  [on_device(): result = jnp.sum(lax.all_gather(part, 'src'), axis=0)]
  transfers between devices with their start and end apart: 4 -> 3, of which waited for: 4 -> 3; matrix products, arithmetic and copies ran while one was open for 2% -> 3% of each run, Pallas kernels for 0% -> 0%
where the time goes in v1:
time: 227 us; the launch traced here: 226 us
  waiting for transfers between devices  153 us (67%)
  blocking collectives  47.1 us (21%)
  between operations  13.1 us (6%)
  matrix products  12.9 us (6%)
    all_gather x1, waiting for transfers between devices, on_device(): acts = lax.all_gather(source_act[0], 'blk', axis=0, tiled=True)  75.3 us
    all_gather x1, blocking collectives, on_device(): probe_rows = lax.all_gather(probes, 'blk', axis=0, tiled=True)  42 us
    all_gather x1, waiting for transfers between devices, on_device(): grads = lax.all_gather(source_grad[0], 'blk', axis=0, tiled=True)  41.9 us
    reduce_scatter x1, waiting for transfers between devices, on_device(): part = lax.psum_scatter(total, 'layer', scatter_dimension=0, tiled=True)  34 us
    dot_general x1, matrix products, on_device(): lax.dot_general(kernel, probe_rows, (((0,), (0,)), ((), ())), preferred_e...  7.07 us
    dot_general x1, matrix products, contract_rows(): lax.dot_general(left, right, (((1,), (1,)), ((), ())), preferred_element_...  5.82 us
    all_gather x1, blocking collectives, on_device(): result = jnp.sum(lax.all_gather(part, 'src'), axis=0)  5.08 us
  transfers between devices with their start and end apart: 3, of which 3 were waited for; matrix products, arithmetic and copies ran while one was open for 3% of the time, Pallas kernels for 0%

profile of v1, /device:TPU:1, one launch (start us, length us, event | category | flops | bytes accessed | tf_op | source)
XLA Modules:
  0.0 226.5 jit_solution(6347251749726440744)
XLA Ops:
  6.5 0.0 all-gather.8.cloned.1.call-start
  6.5 0.7 all-gather.8.cloned.1.call-update
  7.3 0.0 all-gather.6.cloned.1.call-start
  7.3 0.7 all-gather.6.cloned.1.call-update
  8.0 0.0 reduce-scatter.2.cloned.1.call-start
  8.1 42.0 %all_gather.17 = bf16[512,256]{1,0:T(8,128)(2,1)S(1)} all-gather(bf16[16,256]{1,0:T(8,128)(2,1)} %param.9), channel_id=1, replica_groups=mesh['blk'=32,'src'=2,'layer'=4] {'blk'}, dimensions={0}, use_global_device_ids=true | all-gather | bytes 270336 | tf_op jit(solution)/shard_map/all_gather | solution.py:20
  50.0 41.9 %all-gather.8.cloned.1.call-done = bf16[1,512,4096]{2,1,0:T(8,128)(2,1)} async-done(((bf16[1,16,4096]{2,1,0:T(8,128)(2,1)}), bf16[1,512,4096]{2,1,0:T(8,128)(2,1)}) %all-gather.8.cloned.1.call-update) | async-done | bytes 4194320 | tf_op jit(solution)/shard_map/all_gather | solution.py:22
  91.9 5.8 %fusion = f32[512,512]{1,0:T(8,128)S(1)} fusion(bf16[1,512,4096]{2,1,0:T(8,128)(2,1)} %param.6, bf16[1,512,4096]{2,1,0:T(8,128)(2,1)} %all-gather.8.cloned.1.call-done), kind=kOutput, calls=%fused_computation | convolution fusion | flops 2147483648 | bytes 9437184 | tf_op jit(solution)/shard_map/dot_general | solution.py:10
  97.8 75.3 %all-gather.6.cloned.1.call-done = bf16[1,512,4096]{2,1,0:T(8,128)(2,1)} async-done(((bf16[1,16,4096]{2,1,0:T(8,128)(2,1)}), bf16[1,512,4096]{2,1,0:T(8,128)(2,1)}) %all-gather.6.cloned.1.call-update) | async-done | bytes 4194320 | tf_op jit(solution)/shard_map/all_gather | solution.py:21
  173.0 7.1 %fusion.23 = f32[512,256]{1,0:T(8,128)} fusion(bf16[512,256]{1,0:T(8,128)(2,1)S(1)} %all_gather.17, f32[512,512]{1,0:T(8,128)S(1)} %fusion, bf16[1,512,4096]{2,1,0:T(8,128)(2,1)} %param.5, bf16[1,512,4096]{2,1,0:T(8,128)(2,1)} %all-gather.6.cloned.1.call-done), kind=kOutput, calls=%fused_computation.9 | convolution fusion | flops 2282487808 | bytes 10223616 | tf_op jit(solution)/shard_map/dot_general | solution.py:26
  180.1 0.0 reduce-scatter.2.cloned.1.call-update
  180.1 34.0 %reduce-scatter.2.cloned.1.call-done = f32[128,256]{1,0:T(8,128)} async-done(((f32[512,256]{1,0:T(8,128)}), f32[128,256]{1,0:T(8,128)}) %reduce-scatter.2.cloned.1.call-update) | async-done | bytes 131088 | tf_op jit(solution)/shard_map/reduce_scatter | solution.py:29
  214.2 5.1 %all-gather.2 = f32[256,256]{1,0:T(8,128)S(1)} all-gather(f32[128,256]{1,0:T(8,128)} %reduce-scatter.2.cloned.1.call-done), channel_id=4, replica_groups=mesh['blk'=32,'src'=2,'layer'=4] {'src'}, dimensions={0}, use_global_device_ids=true | all-gather | bytes 393216 | tf_op jit(solution)/shard_map/all_gather | solution.py:30
  219.3 0.7 broadcast_multiply_fusion
  (1 shorter events, 0.0 us)
Async XLA Ops:
  6.5 85.4 %all-gather.8.cloned.1.call-start = ((), (), s32[]{:S(2)}) async-start(), calls=%async_computation.3 | async-start | bytes 4325376 | tf_op jit(solution)/shard_map/all_gather | solution.py:22
  7.3 165.8 %all-gather.6.cloned.1.call-start = ((), (), s32[]{:S(2)}) async-start(), calls=%async_computation.2 | async-start | bytes 4325376 | tf_op jit(solution)/shard_map/all_gather | solution.py:21
  8.0 206.1 %reduce-scatter.2.cloned.1.call-start = ((), (), s32[]{:S(2)}) async-start(), calls=%async_computation.1 | async-start | bytes 655360 | tf_op jit(solution)/shard_map/reduce_scatter | solution.py:29
Sparse Core Ops, SparseCore 0:
  9.9 81.9 all-gather.7
  94.5 78.4 all-gather.5
  180.3 33.8 reduce-scatter.1
